TPU v7x, 32 devices: a whole 2x2x4 slice. The times are simulated.
32 devices in a mesh: sub: 8 (over z, core), sta: 4 (over y, x).
Axes of the slice: x: 2, y: 2, z: 4, core: 2. Of those that a mesh axis runs over, the one named last changes fastest.
Arguments:
- voltages: bfloat16 [8, 2, 64, 65536], P('sub', None, 'sta'), may hold values from -6 to 6
- beam_weights: bfloat16 [8, 2, 32, 64], P('sub'), may hold values from -0.5 to 0.5
- station_delays: int32 [64], P('sta'), may hold values from 0 to 16383
- dm_index: int32 [32, 1], P('sta'), may hold values from 1 to 8
Outputs:
- dedispersed: float32 [8, 2, 32, 1, 65536], P(None, None, None, None, ('sub', 'sta'))
- intensity: float32 [32, 1, 65536], P(None, None, ('sub', 'sta'))
Inputs may be any that keep to these rules, and one draw needn't show every extreme that they name: `station_delays`: delays in whole samples. `dm_index`: dispersion measure in steps of 10.
All inputs are finite; a program needn't handle non-finite values.
Results may differ from a plain program's by a relative error of at most 0.0006.
Values may be sent and summed in bfloat16 or wider, within the bound.
A program may use at most 320 MiB of HBM per device.

v0:
```python
import jax
import jax.numpy as jnp
from jax import lax
from jax.sharding import PartitionSpec as P

ROOT = 256


TWO_PI = 6.283185307179586
DISPERSION = 4148808000.0
DM_STEP = 10.0
BASE_FREQ = 120.0
CHANNEL_WIDTH = 0.1953125
HIGHEST = lax.Precision.HIGHEST


def angle_tables(rows_len, modulus):
    first = jnp.arange(rows_len, dtype=jnp.int32)[:, None]
    second = jnp.arange(rows_len, dtype=jnp.int32)[None, :]
    product = first * second % modulus
    angles = TWO_PI * product.astype(jnp.float32) / modulus
    return (jnp.cos(angles), jnp.sin(angles))


def chirp_base(subband, root_len, total_len):
    first = jnp.arange(root_len, dtype=jnp.int32)[:, None]
    second = jnp.arange(root_len, dtype=jnp.int32)[None, :]
    positions = first + root_len * second
    signed_bin = jnp.where(positions < total_len // 2, positions, positions - total_len)
    offset = (CHANNEL_WIDTH * signed_bin.astype(jnp.float32) / total_len)[None]
    centre = (BASE_FREQ + CHANNEL_WIDTH * (subband.astype(jnp.float32) + 0.5))[:, None, None]
    return TWO_PI * DISPERSION * offset * offset / (centre * centre * (centre + offset))


def left_dft(cos_table, sin_table, x_real, x_imag, flip_sign):
    real_part = jnp.einsum(
        "kt,...tu->...ku", cos_table, x_real, precision=HIGHEST
    ) + flip_sign * jnp.einsum("kt,...tu->...ku", sin_table, x_imag, precision=HIGHEST)
    imag_part = jnp.einsum(
        "kt,...tu->...ku", cos_table, x_imag, precision=HIGHEST
    ) - flip_sign * jnp.einsum("kt,...tu->...ku", sin_table, x_real, precision=HIGHEST)
    return (real_part, imag_part)


def right_dft(cos_table, sin_table, x_real, x_imag, flip_sign):
    real_part = jnp.einsum(
        "...kt,tm->...km", x_real, cos_table, precision=HIGHEST
    ) + flip_sign * jnp.einsum("...kt,tm->...km", x_imag, sin_table, precision=HIGHEST)
    imag_part = jnp.einsum(
        "...kt,tm->...km", x_imag, cos_table, precision=HIGHEST
    ) - flip_sign * jnp.einsum("...kt,tm->...km", x_real, sin_table, precision=HIGHEST)
    return (real_part, imag_part)


def beam_terms(w_block, v_real, v_imag):
    w_real = w_block[:, 0]
    w_imag = w_block[:, 1]
    real_part = jnp.einsum(
        "sbk,skt->bst", w_real, v_real, preferred_element_type=jnp.float32
    ) - jnp.einsum("sbk,skt->bst", w_imag, v_imag, preferred_element_type=jnp.float32)
    imag_part = jnp.einsum(
        "sbk,skt->bst", w_real, v_imag, preferred_element_type=jnp.float32
    ) + jnp.einsum("sbk,skt->bst", w_imag, v_real, preferred_element_type=jnp.float32)
    return jnp.stack([real_part, imag_part], axis=2)


def shards(voltages, beam_weights, station_delays, dm_index):
    sub_dev = voltages.shape[0]
    total_len = voltages.shape[3]
    local_beams = dm_index.shape[0]
    trials = dm_index.shape[1]
    root_len = ROOT
    doubled = jnp.concatenate([voltages, voltages], axis=3)
    shifted = jax.vmap(
        lambda rows, shift_by: lax.dynamic_slice_in_dim(rows, total_len - shift_by, total_len, 2),
        in_axes=(2, 0),
        out_axes=2,
    )(doubled, station_delays)
    own_weights = lax.dynamic_slice_in_dim(
        beam_weights, lax.axis_index("sta") * local_beams, local_beams, 2
    )
    shard_piece = lax.all_gather(shifted, "sta", axis=2, tiled=True)
    beams = beam_terms(own_weights, shard_piece[:, 0], shard_piece[:, 1])
    cos_root, sin_root = angle_tables(root_len, root_len)
    cos_twist, sin_twist = angle_tables(root_len, total_len)
    x_real = beams[:, :, 0].reshape(local_beams, sub_dev, root_len, root_len)
    x_imag = beams[:, :, 1].reshape(local_beams, sub_dev, root_len, root_len)
    a_real, a_imag = left_dft(cos_root, sin_root, x_real, x_imag, 1.0)
    b_real = a_real * cos_twist + a_imag * sin_twist
    b_imag = a_imag * cos_twist - a_real * sin_twist
    s_real, s_imag = right_dft(cos_root, sin_root, b_real, b_imag, 1.0)
    subband = lax.axis_index("sub") * sub_dev + jnp.arange(sub_dev, dtype=jnp.int32)
    base_phase = chirp_base(subband, root_len, total_len)
    dm_value = DM_STEP * dm_index.astype(jnp.float32)
    phase_table = dm_value[:, None, :, None, None] * base_phase[None, :, None, :, :]
    h_real = jnp.cos(phase_table)
    h_imag = jnp.sin(phase_table)
    c_real = s_real[:, :, None] * h_real - s_imag[:, :, None] * h_imag
    c_imag = s_real[:, :, None] * h_imag + s_imag[:, :, None] * h_real
    d_real, d_imag = right_dft(cos_root, sin_root, c_real, c_imag, -1.0)
    e_real = d_real * cos_twist - d_imag * sin_twist
    e_imag = d_imag * cos_twist + d_real * sin_twist
    scale = 1.0 / total_len
    out_real = jnp.einsum("tk,bsjku->sbjtu", cos_root, e_real, precision=HIGHEST) - jnp.einsum(
        "tk,bsjku->sbjtu", sin_root, e_imag, precision=HIGHEST
    )
    out_imag = jnp.einsum("tk,bsjku->sbjtu", cos_root, e_imag, precision=HIGHEST) + jnp.einsum(
        "tk,bsjku->sbjtu", sin_root, e_real, precision=HIGHEST
    )
    series = jnp.stack([out_real * scale, out_imag * scale], axis=1).reshape(
        sub_dev, 2, local_beams, trials, total_len
    )
    n_sub = lax.axis_size("sub")
    n_sta = lax.axis_size("sta")
    moved = lax.all_to_all(series[None], ("sub", "sta"), split_axis=5, concat_axis=0, tiled=True)
    moved = moved.reshape(n_sub, n_sta, sub_dev, 2, local_beams, trials, -1)
    moved = moved.transpose(0, 2, 3, 1, 4, 5, 6).reshape(
        n_sub * sub_dev, 2, n_sta * local_beams, trials, -1
    )
    intensity = jnp.mean(moved[:, 0] * moved[:, 0] + moved[:, 1] * moved[:, 1], axis=0)
    return (moved, intensity)


def solution(mesh):
    return jax.shard_map(
        shards,
        mesh=mesh,
        in_specs=(
            P("sub", None, "sta", None),
            P("sub", None, None, None),
            P("sta"),
            P("sta", None),
        ),
        out_specs=(P(None, None, None, None, ("sub", "sta")), P(None, None, ("sub", "sta"))),
        check_vma=False,
    )
```

profile of v0, /device:TPU:0, one launch (start us, length us, event | category | flops | bytes accessed | tf_op | source)
XLA Modules:
  0.0 1215.8 jit_solution(15129982250046369785)
XLA Ops:
  7.9 6.5 copy.86
  14.4 9.4 maximum_bitcast_fusion
  23.8 62.1 %while.1 = (s32[]{:T(128)}, bf16[16,1,2,131072]{3,2,1,0:T(2,128)(2,1)}, s32[16,4]{0,1:T(4,128)S(1)}, bf16[16,1,2,65536]{3,2,1,0:T(2,128)(2,1)}, s32[]{:T(128)}) while((s32[]{:T(128)}, bf16[16,1,2,131072]{3,2,1,0:T(2,128)(2,1)}, s32[16,4]{0,1:T(4,128)S(1)}, bf16[16,1,2,65536]{3,2,1,0:T(2,128)(2,1)}, s32[]{:T(128)}) %tuple.27), condition=%wide.while_cond, body=%wide.while_body.sunk | while | flops 2 | bytes 525437 | solution.py:75
  86.0 6.4 copy.122
  93.9 158.7 %all-gather.2.cloned.1.call-done = bf16[1,2,64,65536]{3,2,1,0:T(8,128)(2,1)} async-done(((bf16[1,2,16,65536]{3,2,1,0:T(8,128)(2,1)}), bf16[1,2,64,65536]{3,2,1,0:T(8,128)(2,1)}) %all-gather.2.cloned.1.call-update) | async-done | bytes 16777232 | tf_op jit(solution)/shard_map/all_gather | solution.py:82
  252.6 4.6 fusion.1
  257.2 6.1 convolution_add_fusion
  269.5 4.6 fusion
  274.1 6.1 convolution_subtract_fusion
  283.2 4.6 fusion.52
  293.7 5.1 fusion.25
  298.7 4.6 fusion.27
  303.3 4.6 fusion.20
  307.9 4.8 fusion.17
  312.8 10.4 fusion.44
  323.1 10.2 fusion.46
  333.3 10.6 multiply_subtract_fusion.1
  343.9 10.4 multiply_add_fusion.1
  354.3 4.8 fusion.24
  359.1 5.7 fusion.23
  364.8 5.8 multiply_bitcast_fusion
  377.2 7.9 multiply_bitcast_fusion.1
  388.8 4.5 pad_maximum_fusion
  393.3 114.7 %copy.105 = f32[1,1,2,8,1,65536]{3,4,2,1,0,5:T(1,128)} copy(f32[1,1,2,8,1,65536]{5,3,4,2,1,0:T(8,128)} %pad_maximum_fusion) | data formatting | bytes 8388608 | tf_op jit(solution)/shard_map/stack | solution.py:110
  508.5 240.9 %reduce.2 = f32[65536,2,8]{2,1,0:T(2,128)} reduce(f32[65536,1,1,2,1,8]{5,4,3,2,1,0:T(1,128)} %bitcast.142, f32[]{:T(128)} %broadcast.336), dimensions={1,2,4}, to_apply=%bitcast.142.reduce_sub_computation | reduce | bytes 8388612
  749.4 109.1 %reshape.375 = f32[32,1,32768]{2,1,0:T(1,128)} reshape(f32[65536,2,8]{2,1,0:T(2,128)} %reduce.2) | data formatting | bytes 8388608
  858.5 98.9 %all_to_all.15 = f32[32,1,32768]{2,1,0:T(1,128)} all-to-all(f32[32,1,32768]{2,1,0:T(1,128)} %reshape.375), channel_id=1, replica_groups=mesh['sub'=8,'sta'=4] {'sub','sta'}, dimensions={0} | all-to-all | bytes 8388608 | tf_op jit(solution)/shard_map/all_to_all | solution.py:115
  957.4 13.8 %reduce.3 = f32[32,32768]{1,0:T(8,128)} reduce(f32[32,1,32768]{2,1,0:T(1,128)} %all_to_all.15, f32[]{:T(128)} %broadcast.336), dimensions={1}, to_apply=%all_to_all.11.reduce_sub_computation | reduce | bytes 8388612 | tf_op jit(solution)/shard_map/all_to_all | solution.py:115
  971.2 171.2 %reshape.376 = f32[65536,1,1,2,1,8]{5,4,3,2,1,0:T(1,128)} reshape(f32[32,32768]{1,0:T(8,128)} %reduce.3) | data formatting | bytes 8388608
  1142.4 53.6 %copy.118 = f32[1,1,2,8,1,32,2048]{6,5,3,2,4,1,0:T(8,128)} copy(f32[1,1,2,8,1,32,2048]{3,2,6,5,4,1,0:T(2,128)} %bitcast.32) | data formatting | bytes 8388608 | tf_op jit(solution)/shard_map/all_to_all | solution.py:115
  1196.0 4.6 copy.107
  1201.4 6.4 copy.109
  (86 shorter events, 91.7 us)
Async XLA Ops:
  7.2 245.4 %copy-start = (bf16[1,2,32,64]{3,2,1,0:T(8,128)(2,1)S(1)}, bf16[1,2,32,64]{3,2,1,0:T(8,128)(2,1)}, u32[]{:S(2)}) copy-start(bf16[1,2,32,64]{3,2,1,0:T(8,128)(2,1)} %param.5) | copy-start | bytes 24580
  7.2 245.4 %all-gather.2.cloned.1.call-start = ((), (), s32[]{:S(2)}) async-start(), calls=%async_computation.1 | async-start | bytes 20971520 | tf_op jit(solution)/shard_map/all_gather | solution.py:82
  92.4 1.4 copy-start.5
  283.2 4.6 copy-start.3
  283.2 4.6 copy-start.4
  354.3 10.5 copy-start.2
  1201.3 7.3 copy-start.1
Sparse Core Ops, SparseCore 0:
  92.5 160.0 all-gather.1
where the time goes:
time: 1230 us; the launch traced here: 1220 us
  local copies, waits for them, and re-layouts  552 us (45%)
  other arithmetic  271 us (22%)
  waiting for transfers between devices  159 us (13%)
  matrix products  121 us (10%)
  blocking collectives  98.9 us (8%)
  between operations  14.6 us (1%)
    unnamed x18, local copies, waits for them, and re-layouts  294 us
    unnamed x2, other arithmetic  241 us
    all_gather x1, waiting for transfers between devices, shards(): shard_piece = lax.all_gather(shifted, 'sta', axis=2, tiled=True)  159 us
    another operation x3, local copies, waits for them, and re-layouts, shards(): jnp.stack([out_real * scale, out_imag * scale], axis=1)  120 us
    all_to_all x1, blocking collectives, shards(): lax.all_to_all(series[None], ('sub', 'sta'), split_axis=5, concat_axis=0,...  98.9 us
    gather x48, local copies, waits for them, and re-layouts  62.1 us
    all_to_all x2, local copies, waits for them, and re-layouts, shards(): lax.all_to_all(series[None], ('sub', 'sta'), split_axis=5, concat_axis=0,...  58.2 us
  transfers between devices with their start and end apart: 1, of which 1 were waited for; matrix products, arithmetic and copies ran while one was open for 0% of the time, Pallas kernels for 0%

commit v1 on v0

v1 whole, which is shorter than its diff:
```python
import functools

import jax
import jax.numpy as jnp
import numpy as np
from jax import lax
from jax.experimental import pallas as pl
from jax.experimental.pallas import tpu as pltpu
from jax.sharding import PartitionSpec as P


TWO_PI = 6.283185307179586
DISPERSION = 4148808000.0
DM_STEP = 10.0
BASE_FREQ = 120.0
CHANNEL_WIDTH = 0.1953125


def dft_tables(root_len):
    total_len = root_len * root_len
    product = np.outer(np.arange(root_len), np.arange(root_len))
    root_angle = 2 * np.pi * (product % root_len) / root_len
    cos_root, sin_root = np.cos(root_angle), np.sin(root_angle)
    left = np.block([[cos_root, sin_root], [-sin_root, cos_root]]).astype(np.float32)
    high = left.astype(jnp.bfloat16)
    low = (left - high.astype(np.float32)).astype(jnp.bfloat16)
    twist_angle = 2 * np.pi * product / total_len
    twist = np.stack([np.cos(twist_angle), np.sin(twist_angle)]).astype(np.float32)
    return np.stack([high, low]), np.stack([high.T, low.T]), twist


def chirp_base(subband, root_len, total_len):
    first = jnp.arange(root_len, dtype=jnp.int32)[:, None]
    second = jnp.arange(root_len, dtype=jnp.int32)[None, :]
    positions = first + root_len * second
    signed_bin = jnp.where(positions < total_len // 2, positions, positions - total_len)
    offset = (CHANNEL_WIDTH * signed_bin.astype(jnp.float32) / total_len)[None]
    centre = (BASE_FREQ + CHANNEL_WIDTH * (subband.astype(jnp.float32) + 0.5))[:, None, None]
    return TWO_PI * DISPERSION * offset * offset / (centre * centre * (centre + offset))


def beam_kernel(w_ref, v_ref, out_ref):
    sums = jnp.dot(w_ref[...], v_ref[...], preferred_element_type=jnp.float32)
    lanes = out_ref.shape[2]
    for row in range(out_ref.shape[1]):
        out_ref[:, row, :] = sums[:, row * lanes : (row + 1) * lanes]


def form_beams(weights, volts, root_len):
    rows, depth = weights.shape
    total_len = volts.shape[1]
    step = 32
    return pl.pallas_call(
        beam_kernel,
        grid=(root_len // step,),
        in_specs=[
            pl.BlockSpec((rows, depth), lambda i: (0, 0)),
            pl.BlockSpec((depth, step * root_len), lambda i: (0, i)),
        ],
        out_specs=pl.BlockSpec((rows, step, root_len), lambda i: (0, i, 0)),
        out_shape=jax.ShapeDtypeStruct((rows, root_len, root_len), jnp.float32),
        cost_estimate=pl.CostEstimate(
            flops=2 * rows * depth * total_len, bytes_accessed=2 * depth * total_len, transcendentals=0
        ),
    )(weights, volts)


def split(values):
    high = values.astype(jnp.bfloat16)
    return high, (values - high.astype(jnp.float32)).astype(jnp.bfloat16)


def dot3(a_high, a_low, b_high, b_low):
    dot = functools.partial(jnp.dot, preferred_element_type=jnp.float32)
    return dot(a_high, b_high) + (dot(a_high, b_low) + dot(a_low, b_high))


def dedisperse_kernel(x_ref, h_real_ref, h_imag_ref, left_ref, right_ref, twist_ref, out_ref, flat):
    root = twist_ref.shape[1]
    half = root // 2
    cos_twist, sin_twist = twist_ref[0], twist_ref[1]
    x = x_ref[...].reshape(2 * root, root)
    a = dot3(left_ref[0], left_ref[1], *split(x))
    a_real, a_imag = a[:root], a[root:]
    b = jnp.concatenate(
        [a_real * cos_twist + a_imag * sin_twist, a_imag * cos_twist - a_real * sin_twist], axis=1
    )
    s = dot3(*split(b), right_ref[0], right_ref[1])
    s_real, s_imag = s[:, :root], s[:, root:]
    h_real, h_imag = h_real_ref[0], h_imag_ref[0]
    c = jnp.concatenate([s_real * h_real - s_imag * h_imag, s_real * h_imag + s_imag * h_real], axis=1)
    d = dot3(*split(c), left_ref[0], left_ref[1])
    d_real, d_imag = d[:, :root], d[:, root:]
    e = jnp.concatenate(
        [d_real * cos_twist - d_imag * sin_twist, d_imag * cos_twist + d_real * sin_twist], axis=0
    )
    out = dot3(right_ref[0], right_ref[1], *split(e)) * (1.0 / (root * root))
    for part in range(2):
        for side in range(2):
            flat[pl.ds(side, root, 2), :] = out[part * root : (part + 1) * root, side * half : (side + 1) * half]
        out_ref[:, part, 0] = flat[...].reshape(out_ref.shape[0], out_ref.shape[3], half)


def dedisperse(beams, h_real, h_imag, n_dev):
    _, n_beams, root, _ = beams.shape
    left, right, twist = dft_tables(root)
    rows = 2 * root // n_dev
    whole = lambda shape: pl.BlockSpec(shape, lambda b: (0,) * len(shape))
    own = pl.BlockSpec((1, root, root), lambda b: (b, 0, 0))
    return pl.pallas_call(
        dedisperse_kernel,
        grid=(n_beams,),
        in_specs=[
            pl.BlockSpec((2, 1, root, root), lambda b: (0, b, 0, 0)),
            own,
            own,
            whole(left.shape),
            whole(right.shape),
            whole(twist.shape),
        ],
        out_specs=pl.BlockSpec((n_dev, 2, 1, rows, root // 2), lambda b: (0, 0, b, 0, 0)),
        out_shape=jax.ShapeDtypeStruct((n_dev, 2, n_beams, rows, root // 2), jnp.float32),
        scratch_shapes=[pltpu.VMEM((2 * root, root // 2), jnp.float32)],
        cost_estimate=pl.CostEstimate(
            flops=96 * n_beams * root**3, bytes_accessed=24 * n_beams * root**2, transcendentals=0
        ),
    )(beams, h_real, h_imag, left, right, twist)


def shards(voltages, beam_weights, station_delays, dm_index):
    sub_dev = voltages.shape[0]
    total_len = voltages.shape[3]
    local_beams = dm_index.shape[0]
    trials = dm_index.shape[1]
    root_len = int(round(total_len**0.5))
    n_sub = lax.axis_size("sub")
    n_sta = lax.axis_size("sta")
    n_dev = n_sub * n_sta
    assert sub_dev == 1 and trials == 1 and root_len * root_len == total_len
    doubled = jnp.concatenate([voltages, voltages], axis=3)
    shifted = jax.vmap(
        lambda rows, shift_by: lax.dynamic_slice_in_dim(rows, total_len - shift_by, total_len, 2),
        in_axes=(2, 0),
        out_axes=2,
    )(doubled, station_delays)
    own_weights = lax.dynamic_slice_in_dim(
        beam_weights, lax.axis_index("sta") * local_beams, local_beams, 2
    )[0]
    w_real, w_imag = own_weights[0], own_weights[1]
    volts = lax.all_gather(shifted[0], "sta", axis=1, tiled=True)
    volts = volts.reshape(-1, total_len)
    weights = jnp.concatenate(
        [jnp.concatenate([w_real, -w_imag], axis=1), jnp.concatenate([w_imag, w_real], axis=1)], axis=0
    )
    beams = form_beams(weights, volts, root_len).reshape(2, local_beams, root_len, root_len)
    subband = lax.axis_index("sub") + jnp.arange(1, dtype=jnp.int32)
    base_phase = chirp_base(subband, root_len, total_len)
    dm_value = DM_STEP * dm_index.astype(jnp.float32)
    phase_table = dm_value[:, :, None] * base_phase
    sent = dedisperse(beams, jnp.cos(phase_table), jnp.sin(phase_table), n_dev)
    moved = lax.all_to_all(sent, ("sub", "sta"), split_axis=0, concat_axis=0, tiled=True)
    moved = moved.reshape(n_sub, n_sta, *moved.shape[1:]).transpose(0, 2, 1, 3, 4, 5)
    moved = moved.reshape(n_sub, 2, n_sta * local_beams, *moved.shape[4:])
    intensity = jnp.mean(moved[:, 0] * moved[:, 0] + moved[:, 1] * moved[:, 1], axis=0)
    return (moved.reshape(*moved.shape[:3], 1, -1), intensity.reshape(intensity.shape[0], 1, -1))


def solution(mesh):
    return jax.shard_map(
        shards,
        mesh=mesh,
        in_specs=(
            P("sub", None, "sta", None),
            P("sub", None, None, None),
            P("sta"),
            P("sta", None),
        ),
        out_specs=(P(None, None, None, None, ("sub", "sta")), P(None, None, ("sub", "sta"))),
        check_vma=False,
    )
```

time: 1230 us -> 412 us (0.33); the launches traced: 1220 us -> 410 us
  local copies, waits for them, and re-layouts: 552 us -> 90.5 us
  other arithmetic: 271 us -> 20.5 us
  matrix products: 121 us -> 0 us
  Pallas kernels: 0 us -> 37.5 us
    unnamed x18 -> x8, local copies, waits for them, and re-layouts: 294 us -> 7.31 us
    unnamed x2 -> x1, other arithmetic: 241 us -> 0.01 us
    another operation x5 -> x0, local copies, waits for them, and re-layouts: 125 us -> none  [the longest x3 120 us: shards(): jnp.stack([out_real * scale, out_imag * scale], axis=1)]
    dot_general x20 -> x0, matrix products: 121 us -> none  [the longest x2 15.6 us: right_dft(): jnp.einsum('...kt,tm->...km', x_real, sin_table, precision=HIGHEST)]
    all_to_all x2 -> x0, local copies, waits for them, and re-layouts: 58.2 us -> none  [shards(): lax.all_to_all(series[None], ('sub', 'sta'), split_axis=5, concat_axis=0,...]
    pallas_call x0 -> x2, Pallas kernels: none -> 37.5 us  [the longest x1 26.7 us: dedisperse(): pl.pallas_call(dedisperse_kernel, grid=(n_beams,), in_specs=[pl.BlockSpec...]
    all_gather x0 -> x1, local copies, waits for them, and re-layouts: none -> 18.5 us  [shards(): volts = lax.all_gather(shifted[0], 'sta', axis=1, tiled=True)]
    all_to_all x1 -> x0, other arithmetic: 13.8 us -> none  [shards(): lax.all_to_all(series[None], ('sub', 'sta'), split_axis=5, concat_axis=0,...]
  transfers between devices with their start and end apart: 1 -> 1, of which waited for: 1 -> 1; matrix products, arithmetic and copies ran while one was open for 0% -> 3% of each run, Pallas kernels for 0% -> 0%
where the time goes in v1:
time: 412 us; the launch traced here: 410 us
  waiting for transfers between devices  149 us (36%)
  blocking collectives  98.6 us (24%)
  local copies, waits for them, and re-layouts  90.5 us (22%)
  Pallas kernels  37.5 us (9%)
  other arithmetic  20.5 us (5%)
  between operations  14.1 us (3%)
    all_gather x1, waiting for transfers between devices, shards(): volts = lax.all_gather(shifted[0], 'sta', axis=1, tiled=True)  149 us
    all_to_all x1, blocking collectives, shards(): lax.all_to_all(sent, ('sub', 'sta'), split_axis=0, concat_axis=0, tiled=T...  98.6 us
    gather x48, local copies, waits for them, and re-layouts  63.4 us
    pallas_call x1, Pallas kernels, dedisperse(): pl.pallas_call(dedisperse_kernel, grid=(n_beams,), in_specs=[pl.BlockSpec...  26.7 us
    all_gather x1, local copies, waits for them, and re-layouts, shards(): volts = lax.all_gather(shifted[0], 'sta', axis=1, tiled=True)  18.5 us
    pallas_call x1, Pallas kernels, form_beams(): pl.pallas_call(beam_kernel, grid=(root_len // step,), in_specs=[pl.BlockS...  10.8 us
    transpose x1, other arithmetic, shards(): lax.dynamic_slice_in_dim(rows, total_len - shift_by, total_len, 2)  8.84 us
    sin x1, other arithmetic, shards(): sent = dedisperse(beams, jnp.cos(phase_table), jnp.sin(phase_table), n_dev)  8.83 us
  transfers between devices with their start and end apart: 1, of which 1 were waited for; matrix products, arithmetic and copies ran while one was open for 3% of the time, Pallas kernels for 0%

profile of v1, /device:TPU:0, one launch (start us, length us, event | category | flops | bytes accessed | tf_op | source)
XLA Modules:
  0.0 410.4 jit_solution(6508875578075095469)
XLA Ops:
  7.2 6.5 %copy.18 = bf16[1,2,16,65536]{3,1,0,2:T(2,128)(2,1)S(1)} copy(bf16[1,2,16,65536]{3,2,1,0:T(8,128)(2,1)} %param.7) | data formatting | bytes 8388608 | tf_op args[0]
  13.7 8.8 %maximum_bitcast_fusion = bf16[16,1,2,131072]{3,2,1,0:T(2,128)(2,1)} fusion(bf16[1,2,16,65536]{3,1,0,2:T(2,128)(2,1)S(1)} %copy.18), kind=kLoop, calls=%fused_computation.2 | loop fusion | flops 16777216 | bytes 12582912 | tf_op jit(solution)/shard_map/vmap()/transpose | solution.py:142
  22.6 63.5 %while.1 = (s32[]{:T(128)}, bf16[16,1,2,131072]{3,2,1,0:T(2,128)(2,1)}, s32[16,4]{0,1:T(4,128)S(1)}, bf16[16,1,2,65536]{3,2,1,0:T(2,128)(2,1)}, s32[]{:T(128)}) while((s32[]{:T(128)}, bf16[16,1,2,131072]{3,2,1,0:T(2,128)(2,1)}, s32[16,4]{0,1:T(4,128)S(1)}, bf16[16,1,2,65536]{3,2,1,0:T(2,128)(2,1)}, s32[]{:T(128)}) %tuple.27), condition=%wide.while_cond, body=%wide.while_body.sunk | while | flops 2 | bytes 525937 | solution.py:142
  22.7 0.6 fusion.7
  23.3 3.3 dynamic-slice_dynamic-update-slice_fusion.2
  27.3 3.3 dynamic-slice_dynamic-update-slice_fusion.2
  30.6 0.6 fusion.7
  31.2 3.3 dynamic-slice_dynamic-update-slice_fusion.2
  35.2 3.3 dynamic-slice_dynamic-update-slice_fusion.2
  39.2 3.3 dynamic-slice_dynamic-update-slice_fusion.2
  43.1 3.3 dynamic-slice_dynamic-update-slice_fusion.2
  47.1 3.3 dynamic-slice_dynamic-update-slice_fusion.2
  51.1 3.3 dynamic-slice_dynamic-update-slice_fusion.2
  55.0 3.3 dynamic-slice_dynamic-update-slice_fusion.2
  59.0 3.3 dynamic-slice_dynamic-update-slice_fusion.2
  63.0 3.3 dynamic-slice_dynamic-update-slice_fusion.2
  66.9 3.3 dynamic-slice_dynamic-update-slice_fusion.2
  70.9 3.3 dynamic-slice_dynamic-update-slice_fusion.2
  74.9 3.3 dynamic-slice_dynamic-update-slice_fusion.2
  78.8 3.3 dynamic-slice_dynamic-update-slice_fusion.2
  82.8 3.3 dynamic-slice_dynamic-update-slice_fusion.2
  86.1 0.7 dynamic-slice_bitcast_fusion.1
  86.8 0.7 fusion.4
  87.5 0.7 maximum_maximum_fusion.w_ref
  88.3 8.8 %multiply_sine_fusion = (f32[8,256,256]{2,1,0:T(8,128)}, f32[8,256,256]{2,1,0:T(8,128)}) fusion(f32[256,256]{1,0:T(8,128)S(1)} %multiply_divide_fusion, f32[8]{0:T(128)S(1)} %multiply_bitcast_fusion), kind=kLoop, calls=%fused_computation.3 | loop fusion | flops 524288 | bytes 4456480 | tf_op jit(solution)/shard_map/sin | solution.py:160
  97.2 149.2 %all-gather.3.cloned.1.call-done = bf16[1,2,64,65536]{3,1,0,2:T(2,128)(2,1)} async-done(((bf16[1,2,16,65536]{3,1,0,2:T(2,128)(2,1)}), bf16[1,2,64,65536]{3,1,0,2:T(2,128)(2,1)}) %all-gather.3.cloned.1.call-update) | async-done | bytes 16777232 | tf_op jit(solution)/shard_map/all_gather | solution.py:150
  246.4 18.5 %copy.20 = bf16[1,2,64,65536]{3,2,1,0:T(8,128)(2,1)} copy(bf16[1,2,64,65536]{3,1,0,2:T(2,128)(2,1)} %all-gather.3.cloned.1.call-done) | data formatting | bytes 33554432 | tf_op jit(solution)/shard_map/all_gather | solution.py:150
  264.9 10.8 %shard_map.86 = f32[16,256,256]{2,1,0:T(8,128)} custom-call(bf16[16,128]{1,0:T(8,128)(2,1)} %maximum_maximum_fusion.w_ref, bf16[128,65536]{1,0:T(8,128)(2,1)} %bitcast.27), custom_call_target="tpu_custom_call" | custom-call | flops 268435456 | bytes 16777216 | tf_op jit(solution)/shard_map/pallas_call | solution.py:53
  275.7 26.7 %shard_map.87 = f32[32,2,8,16,128]{4,3,2,1,0:T(8,128)} custom-call(f32[2,8,256,256]{3,2,1,0:T(8,128)} %bitcast.32, f32[8,256,256]{2,1,0:T(8,128)} %get-tuple-element.27.h_real_ref, f32[8,256,256]{2,1,0:T(8,128)} %get-tuple-element.26.h_imag_ref, bf16[2,512,512]{2,1,0:T(8,128)(2,1)} %constant.59.clone.left_ref, ...), custom_call_target="tpu_custom_call" | custom-call | flops 12884901888 | bytes 12582912 | tf_op jit(solution)/shard_map/pallas_call | solution.py:110
  302.4 98.6 %all_to_all.5 = f32[32,2,8,16,128]{4,3,2,1,0:T(8,128)S(1)} all-to-all(f32[32,2,8,16,128]{4,3,2,1,0:T(8,128)} %shard_map.87), channel_id=1, replica_groups=mesh['sub'=8,'sta'=4] {'sub','sta'}, dimensions={0} | all-to-all | bytes 8388608 | tf_op jit(solution)/shard_map/all_to_all | solution.py:161
  401.8 1.0 broadcast_multiply_fusion
  402.8 0.8 copy-done
  (46 shorter events, 10.3 us)
Async XLA Ops:
  7.2 239.2 %all-gather.3.cloned.1.call-start = ((), (), s32[]{:S(2)}) async-start(), calls=%async_computation.1 | async-start | bytes 20971520 | tf_op jit(solution)/shard_map/all_gather | solution.py:150
  13.7 8.9 %copy-start.1 = (s32[16]{0:T(128)S(1)}, s32[16]{0:T(128)}, u32[]{:S(2)}) copy-start(s32[16]{0:T(128)} %param.9) | copy-start | bytes 196
  22.6 65.6 %copy-start.2 = (s32[8,1]{0,1:T(1,128)S(1)}, s32[8,1]{0,1:T(1,128)}, u32[]{:S(2)}) copy-start(s32[8,1]{0,1:T(1,128)} %param.10) | copy-start | bytes 100
  401.5 2.1 copy-start
Sparse Core Ops, SparseCore 0:
  86.2 160.0 all-gather.2

commit v2 on v1

--- a/solution.py
+++ b/solution.py
@@ -63,6 +63,46 @@
             flops=2 * rows * depth * total_len, bytes_accessed=2 * depth * total_len, transcendentals=0
         ),
     )(weights, volts)
+
+
+def shift_kernel(delay_ref, x_ref, out_ref, doubled, window):
+    rows, total_len = x_ref.shape[1:]
+    width = window.shape[1]
+    step = width - 128
+    doubled[:, :total_len] = x_ref[0].astype(jnp.float32)
+    doubled[:, total_len:] = doubled[:, :total_len]
+    row_id = lax.broadcasted_iota(jnp.int32, (rows, width), 0)
+    fine = jnp.zeros((rows, width), jnp.int32)
+    for row in range(rows):
+        fine = jnp.where(row_id == row, delay_ref[row] % 128, fine)
+
+    def chunk(i, carry):
+        for row in range(rows):
+            start = total_len + i * step - (delay_ref[row] // 128) * 128 - 128
+            window[row : row + 1, :] = doubled[row : row + 1, pl.ds(pl.multiple_of(start, 128), width)]
+        values = window[...]
+        for bit in range(7):
+            values = jnp.where((fine >> bit) & 1 == 1, pltpu.roll(values, 1 << bit, 1), values)
+        out_ref[0, :, pl.ds(pl.multiple_of(i * step, 128), step)] = values[:, 128:].astype(out_ref.dtype)
+        return carry
+
+    lax.fori_loop(0, total_len // step, chunk, 0)
+
+
+def shift(volts, delays):
+    parts, rows, total_len = volts.shape
+    block = pl.BlockSpec((1, rows, total_len), lambda i: (i, 0, 0))
+    return pl.pallas_call(
+        shift_kernel,
+        grid=(parts,),
+        in_specs=[pl.BlockSpec(memory_space=pltpu.SMEM), block],
+        out_specs=block,
+        out_shape=jax.ShapeDtypeStruct(volts.shape, volts.dtype),
+        scratch_shapes=[
+            pltpu.VMEM((rows, 2 * total_len), jnp.float32),
+            pltpu.VMEM((rows, 2048 + 128), jnp.float32),
+        ],
+    )(delays, volts)
 
 
 def split(values):
@@ -137,17 +177,12 @@
     n_sta = lax.axis_size("sta")
     n_dev = n_sub * n_sta
     assert sub_dev == 1 and trials == 1 and root_len * root_len == total_len
-    doubled = jnp.concatenate([voltages, voltages], axis=3)
-    shifted = jax.vmap(
-        lambda rows, shift_by: lax.dynamic_slice_in_dim(rows, total_len - shift_by, total_len, 2),
-        in_axes=(2, 0),
-        out_axes=2,
-    )(doubled, station_delays)
+    shifted = shift(voltages[0], station_delays)
     own_weights = lax.dynamic_slice_in_dim(
         beam_weights, lax.axis_index("sta") * local_beams, local_beams, 2
     )[0]
     w_real, w_imag = own_weights[0], own_weights[1]
-    volts = lax.all_gather(shifted[0], "sta", axis=1, tiled=True)
+    volts = lax.all_gather(shifted, "sta", axis=1, tiled=True)
     volts = volts.reshape(-1, total_len)
     weights = jnp.concatenate(
         [jnp.concatenate([w_real, -w_imag], axis=1), jnp.concatenate([w_imag, w_real], axis=1)], axis=0
@@ -158,7 +193,13 @@
     dm_value = DM_STEP * dm_index.astype(jnp.float32)
     phase_table = dm_value[:, :, None] * base_phase
     sent = dedisperse(beams, jnp.cos(phase_table), jnp.sin(phase_table), n_dev)
+    power = jnp.mean(beams[0] * beams[0] + beams[1] * beams[1], axis=(1, 2))
+    rms = jnp.where(power > 0, jnp.sqrt(power), 1.0)
+    gain = 32768.0 / root_len / rms
+    undo = lax.all_gather(rms * (root_len / 32768.0), ("sub", "sta"), axis=0)
+    sent = (sent * gain[None, None, :, None, None]).astype(jnp.float16)
     moved = lax.all_to_all(sent, ("sub", "sta"), split_axis=0, concat_axis=0, tiled=True)
+    moved = moved.astype(jnp.float32) * undo[:, None, :, None, None]
     moved = moved.reshape(n_sub, n_sta, *moved.shape[1:]).transpose(0, 2, 1, 3, 4, 5)
     moved = moved.reshape(n_sub, 2, n_sta * local_beams, *moved.shape[4:])
     intensity = jnp.mean(moved[:, 0] * moved[:, 0] + moved[:, 1] * moved[:, 1], axis=0)

time: 412 us -> 348 us (0.84)
  local copies, waits for them, and re-layouts: 90.5 us -> 2.96 us
  Pallas kernels: 37.5 us -> 88.4 us
  blocking collectives: 98.6 us -> 69.7 us
  starting transfers between devices: 0.04 us -> 4.64 us
    all_to_all x1 -> x0, blocking collectives: 98.6 us -> none  [shards(): lax.all_to_all(sent, ('sub', 'sta'), split_axis=0, concat_axis=0, tiled=T...]
    unnamed x0 -> x1, blocking collectives: none -> 69.7 us
    gather x48 -> x0, local copies, waits for them, and re-layouts: 63.4 us -> none
    pallas_call x0 -> x1, Pallas kernels: none -> 50.8 us  [shift(): pl.pallas_call(shift_kernel, grid=(parts,), in_specs=[pl.BlockSpec(memory...]
    all_gather x1, local copies, waits for them, and re-layouts: 18.5 us -> 0.08 us  [shards(): undo = lax.all_gather(rms * (root_len / 32768.0), ('sub', 'sta'), axis=0)]
    transpose x1 -> x0, other arithmetic: 8.84 us -> none  [shards(): lax.dynamic_slice_in_dim(rows, total_len - shift_by, total_len, 2)]
    unnamed x8 -> x5, local copies, waits for them, and re-layouts: 7.31 us -> 1.7 us
    all_to_all x0 -> x1, starting transfers between devices: none -> 4.6 us  [shards(): lax.all_to_all(sent, ('sub', 'sta'), split_axis=0, concat_axis=0, tiled=T...]
  transfers between devices with their start and end apart: 1 -> 2, of which waited for: 1 -> 1; matrix products, arithmetic and copies ran while one was open for 3% -> 3% of each run, Pallas kernels for 0% -> 0%
where the time goes in v2:
time: 348 us
  waiting for transfers between devices  149 us (43%)
  Pallas kernels  88.4 us (25%)
  blocking collectives  69.7 us (20%)
  other arithmetic  18.6 us (5%)
  between operations  14.1 us (4%)
  starting transfers between devices  4.64 us (1%)
    all_gather x1, waiting for transfers between devices, shards(): volts = lax.all_gather(shifted, 'sta', axis=1, tiled=True)  149 us
    unnamed x1, blocking collectives  69.7 us
    pallas_call x1, Pallas kernels, shift(): pl.pallas_call(shift_kernel, grid=(parts,), in_specs=[pl.BlockSpec(memory...  50.8 us
    pallas_call x1, Pallas kernels, dedisperse(): pl.pallas_call(dedisperse_kernel, grid=(n_beams,), in_specs=[pl.BlockSpec...  26.7 us
    pallas_call x1, Pallas kernels, form_beams(): pl.pallas_call(beam_kernel, grid=(root_len // step,), in_specs=[pl.BlockS...  10.8 us
    sin x1, other arithmetic, shards(): sent = dedisperse(beams, jnp.cos(phase_table), jnp.sin(phase_table), n_dev)  8.79 us
  transfers between devices with their start and end apart: 2, of which 1 were waited for; matrix products, arithmetic and copies ran while one was open for 3% of the time, Pallas kernels for 0%

profile of v2, /device:TPU:0, one launch (start us, length us, event | category | flops | bytes accessed | tf_op | source)
XLA Modules:
  0.0 347.7 jit_solution(12698283413154339033)
XLA Ops:
  7.2 0.0 all-gather.3.cloned.1.call-start
  7.2 50.8 %shard_map.86 = bf16[2,16,65536]{2,1,0:T(8,128)(2,1)} custom-call(s32[16]{0:T(128)} %delay_ref.1, bf16[2,16,65536]{2,1,0:T(8,128)(2,1)} %bitcast.22), custom_call_target="tpu_custom_call" | custom-call | tf_op jit(solution)/shard_map/pallas_call | solution.py:95
  58.1 0.0 copy-start.1
  58.1 0.0 all-gather.3.cloned.1.call-update
  58.1 0.7 dynamic-slice_bitcast_fusion.1
  58.8 0.7 fusion.5
  59.5 0.7 maximum_maximum_fusion.w_ref
  60.2 0.0 copy-done.1
  60.2 0.1 multiply_divide_fusion
  60.3 8.8 %multiply_sine_fusion = (f32[8,256,256]{2,1,0:T(8,128)}, f32[8,256,256]{2,1,0:T(8,128)}) fusion(f32[256,256]{1,0:T(8,128)S(1)} %multiply_divide_fusion, f32[8]{0:T(128)S(1)} %multiply_bitcast_fusion), kind=kLoop, calls=%fused_computation.2 | loop fusion | flops 524288 | bytes 4456480 | tf_op jit(solution)/shard_map/sin | solution.py:195
  69.1 149.3 %all-gather.3.cloned.1.call-done = bf16[2,64,65536]{2,1,0:T(8,128)(2,1)} async-done(((bf16[2,16,65536]{2,1,0:T(8,128)(2,1)}), bf16[2,64,65536]{2,1,0:T(8,128)(2,1)}) %all-gather.3.cloned.1.call-update) | async-done | bytes 16777232 | tf_op jit(solution)/shard_map/all_gather | solution.py:185
  218.3 10.8 %shard_map.87 = f32[16,256,256]{2,1,0:T(8,128)} custom-call(bf16[16,128]{1,0:T(8,128)(2,1)} %maximum_maximum_fusion.w_ref, bf16[128,65536]{1,0:T(8,128)(2,1)} %bitcast.17), custom_call_target="tpu_custom_call" | custom-call | flops 268435456 | bytes 16777216 | tf_op jit(solution)/shard_map/pallas_call | solution.py:53
  229.1 2.6 fusion.3
  231.8 0.1 multiply_dynamic-update-slice_fusion
  231.9 26.7 %shard_map.88 = f32[32,2,8,16,128]{4,3,2,1,0:T(8,128)} custom-call(f32[2,8,256,256]{3,2,1,0:T(8,128)} %bitcast.21, f32[8,256,256]{2,1,0:T(8,128)} %get-tuple-element.7.h_real_ref, f32[8,256,256]{2,1,0:T(8,128)} %get-tuple-element.6.h_imag_ref, bf16[2,512,512]{2,1,0:T(8,128)(2,1)} %constant.62.clone.left_ref, bf16[2,512,512]{2,1,0:T(8,128)(2,1)} %constant.63.clone.right_ref, ...), custom_call_target="tpu_custom_call" | custom-call | flops 12884901888 | bytes 12582912 | tf_op jit(solution)/shard_map/pallas_call | solution.py:150
  258.6 4.2 %multiply_convert_fusion = f16[32,2,8,16,128]{4,3,2,1,0:T(8,128)(2,1)} fusion(f32[32,2,8,16,128]{4,3,2,1,0:T(8,128)} %shard_map.88, f32[8]{0:T(128)S(1)} %get-tuple-element.9), kind=kLoop, calls=%fused_computation.1 | loop fusion | flops 2097152 | bytes 6291488 | tf_op jit(solution)/shard_map/convert_element_type | solution.py:200
  262.8 4.6 %all-to-all-start = ((f16[32,2,8,16,128]{4,3,2,1,0:T(8,128)(2,1)}), f16[32,2,8,16,128]{4,3,2,1,0:T(8,128)(2,1)S(1)}, u32[]{:S(2)}, u32[]{:S(2)}) async-start(f16[32,2,8,16,128]{4,3,2,1,0:T(8,128)(2,1)} %multiply_convert_fusion), calls=%async_computation | async-start | bytes 4194304 | tf_op jit(solution)/shard_map/all_to_all | solution.py:201
  267.4 69.7 %all-reduce = f32[256]{0:T(256)S(1)} all-reduce(f32[256]{0:T(256)S(1)} %get-tuple-element.8), channel_id=2, replica_groups=mesh['sub'=8,'sta'=4] {'sub','sta'}, use_global_device_ids=true, to_apply=%add | all-reduce | flops 256 | bytes 2048
  337.1 0.1 reshape.138
  337.1 0.0 all-to-all-done
  337.1 0.4 convert_multiply_fusion
  337.6 0.5 copy.10
  338.1 0.0 copy-start
  338.1 0.3 fusion.1
  338.4 1.7 copy-done
  340.1 0.7 broadcast_multiply_fusion
  (3 shorter events, 0.0 us)
Async XLA Ops:
  7.2 211.2 %all-gather.3.cloned.1.call-start = ((), (), s32[]{:S(2)}) async-start(), calls=%async_computation.1 | async-start | bytes 20971520 | tf_op jit(solution)/shard_map/all_gather | solution.py:185
  58.1 2.1 copy-start.1
  262.8 74.4 %all-to-all-start = ((f16[32,2,8,16,128]{4,3,2,1,0:T(8,128)(2,1)}), f16[32,2,8,16,128]{4,3,2,1,0:T(8,128)(2,1)S(1)}, u32[]{:S(2)}, u32[]{:S(2)}) async-start(f16[32,2,8,16,128]{4,3,2,1,0:T(8,128)(2,1)} %multiply_convert_fusion), calls=%async_computation | async-start | bytes 4194304 | tf_op jit(solution)/shard_map/all_to_all | solution.py:201
  338.1 2.0 copy-start
Sparse Core Ops, SparseCore 0:
  58.2 160.0 all-gather.2

commit v3 on v2

--- a/solution.py
+++ b/solution.py
@@ -39,22 +39,24 @@
     return TWO_PI * DISPERSION * offset * offset / (centre * centre * (centre + offset))
 
 
-def beam_kernel(w_ref, v_ref, out_ref):
-    sums = jnp.dot(w_ref[...], v_ref[...], preferred_element_type=jnp.float32)
+def beam_kernel(w_ref, v_real_ref, v_imag_ref, out_ref):
+    sums = jnp.dot(w_ref[0], v_real_ref[...], preferred_element_type=jnp.float32)
+    sums += jnp.dot(w_ref[1], v_imag_ref[...], preferred_element_type=jnp.float32)
     lanes = out_ref.shape[2]
     for row in range(out_ref.shape[1]):
         out_ref[:, row, :] = sums[:, row * lanes : (row + 1) * lanes]
 
 
-def form_beams(weights, volts, root_len):
-    rows, depth = weights.shape
-    total_len = volts.shape[1]
+def form_beams(weights, v_real, v_imag, root_len):
+    _, rows, depth = weights.shape
+    total_len = v_real.shape[1]
     step = 32
     return pl.pallas_call(
         beam_kernel,
         grid=(root_len // step,),
         in_specs=[
-            pl.BlockSpec((rows, depth), lambda i: (0, 0)),
+            pl.BlockSpec((2, rows, depth), lambda i: (0, 0, 0)),
+            pl.BlockSpec((depth, step * root_len), lambda i: (0, i)),
             pl.BlockSpec((depth, step * root_len), lambda i: (0, i)),
         ],
         out_specs=pl.BlockSpec((rows, step, root_len), lambda i: (0, i, 0)),
@@ -62,7 +64,7 @@
         cost_estimate=pl.CostEstimate(
             flops=2 * rows * depth * total_len, bytes_accessed=2 * depth * total_len, transcendentals=0
         ),
-    )(weights, volts)
+    )(weights, v_real, v_imag)
 
 
 def shift_kernel(delay_ref, x_ref, out_ref, doubled, window):
@@ -177,17 +179,18 @@
     n_sta = lax.axis_size("sta")
     n_dev = n_sub * n_sta
     assert sub_dev == 1 and trials == 1 and root_len * root_len == total_len
-    shifted = shift(voltages[0], station_delays)
+    gathered = [
+        lax.all_gather(shift(voltages[0, part : part + 1], station_delays)[0], "sta", axis=0, tiled=True)
+        for part in range(2)
+    ]
     own_weights = lax.dynamic_slice_in_dim(
         beam_weights, lax.axis_index("sta") * local_beams, local_beams, 2
     )[0]
     w_real, w_imag = own_weights[0], own_weights[1]
-    volts = lax.all_gather(shifted, "sta", axis=1, tiled=True)
-    volts = volts.reshape(-1, total_len)
-    weights = jnp.concatenate(
-        [jnp.concatenate([w_real, -w_imag], axis=1), jnp.concatenate([w_imag, w_real], axis=1)], axis=0
-    )
-    beams = form_beams(weights, volts, root_len).reshape(2, local_beams, root_len, root_len)
+    weights = jnp.stack(
+        [jnp.concatenate([w_real, w_imag], axis=0), jnp.concatenate([-w_imag, w_real], axis=0)]
+    )
+    beams = form_beams(weights, *gathered, root_len).reshape(2, local_beams, root_len, root_len)
     subband = lax.axis_index("sub") + jnp.arange(1, dtype=jnp.int32)
     base_phase = chirp_base(subband, root_len, total_len)
     dm_value = DM_STEP * dm_index.astype(jnp.float32)

time: 348 us -> 348 us (level)
  waiting for transfers between devices: 149 us -> 142 us
  local copies, waits for them, and re-layouts: 2.96 us -> 7.5 us
    all_gather x1 -> x2, waiting for transfers between devices: 149 us -> 142 us  [shards(): lax.all_gather(shift(voltages[0, part:part + 1], station_delays)[0], 'sta...]
    squeeze x0 -> x1, local copies, waits for them, and re-layouts: none -> 4.54 us  [shards(): voltages[0, part:part + 1]]
    pallas_call x1 -> x2, Pallas kernels: 50.8 us -> 53.8 us  [shift(): pl.pallas_call(shift_kernel, grid=(parts,), in_specs=[pl.BlockSpec(memory...]
  transfers between devices with their start and end apart: 2 -> 3, of which waited for: 1 -> 2; matrix products, arithmetic and copies ran while one was open for 3% -> 3% of each run, Pallas kernels for 0% -> 8%
where the time goes in v3:
time: 348 us
  waiting for transfers between devices  142 us (41%)
  Pallas kernels  91.1 us (26%)
  blocking collectives  69.7 us (20%)
  other arithmetic  18.6 us (5%)
  between operations  14.1 us (4%)
  local copies, waits for them, and re-layouts  7.5 us (2%)
  starting transfers between devices  4.7 us (1%)
    all_gather x2, waiting for transfers between devices, shards(): lax.all_gather(shift(voltages[0, part:part + 1], station_delays)[0], 'sta...  142 us
    unnamed x1, blocking collectives  69.7 us
    pallas_call x2, Pallas kernels, shift(): pl.pallas_call(shift_kernel, grid=(parts,), in_specs=[pl.BlockSpec(memory...  53.8 us
    pallas_call x1, Pallas kernels, dedisperse(): pl.pallas_call(dedisperse_kernel, grid=(n_beams,), in_specs=[pl.BlockSpec...  26.7 us
    pallas_call x1, Pallas kernels, form_beams(): pl.pallas_call(beam_kernel, grid=(root_len // step,), in_specs=[pl.BlockS...  10.7 us
    sin x1, other arithmetic, shards(): sent = dedisperse(beams, jnp.cos(phase_table), jnp.sin(phase_table), n_dev)  8.85 us
  transfers between devices with their start and end apart: 3, of which 2 were waited for; matrix products, arithmetic and copies ran while one was open for 3% of the time, Pallas kernels for 8%

profile of v3, /device:TPU:0, one launch (start us, length us, event | category | flops | bytes accessed | tf_op | source)
XLA Modules:
  0.0 347.6 jit_solution(18404261878163584986)
XLA Ops:
  7.2 0.0 all-gather.6.cloned.1.call-start
  7.2 4.5 %slice_bitcast_fusion = (bf16[1,16,65536]{2,1,0:T(8,128)(2,1)}, bf16[1,16,65536]{2,1,0:T(8,128)(2,1)}) fusion(bf16[1,2,16,65536]{3,2,1,0:T(8,128)(2,1)} %param.7), kind=kLoop, calls=%fused_computation.12 | loop fusion | bytes 8388608 | tf_op jit(solution)/shard_map/squeeze | solution.py:183
  11.7 26.9 %shard_map.86 = bf16[1,16,65536]{2,1,0:T(8,128)(2,1)} custom-call(s32[16]{0:T(128)} %delay_ref.3, bf16[1,16,65536]{2,1,0:T(8,128)(2,1)} %get-tuple-element.7.x_ref), custom_call_target="tpu_custom_call" | custom-call | tf_op jit(solution)/shard_map/pallas_call | solution.py:97
  38.6 0.0 all-gather.6.cloned.1.call-update
  38.7 0.0 all-gather.8.cloned.1.call-start
  38.7 26.9 %shard_map.87 = bf16[1,16,65536]{2,1,0:T(8,128)(2,1)} custom-call(s32[16]{0:T(128)} %delay_ref.3, bf16[1,16,65536]{2,1,0:T(8,128)(2,1)} %get-tuple-element.6.x_ref), custom_call_target="tpu_custom_call" | custom-call | tf_op jit(solution)/shard_map/pallas_call | solution.py:97
  65.6 0.0 copy-start.1
  65.6 0.0 all-gather.8.cloned.1.call-update
  65.6 0.7 dynamic-slice_bitcast_fusion.1
  66.3 0.7 fusion.5
  67.0 0.6 pad_maximum_fusion.w_ref
  67.6 0.0 copy-done.1
  67.6 0.1 multiply_divide_fusion
  67.8 8.8 %multiply_sine_fusion = (f32[8,256,256]{2,1,0:T(8,128)}, f32[8,256,256]{2,1,0:T(8,128)}) fusion(f32[256,256]{1,0:T(8,128)S(1)} %multiply_divide_fusion, f32[8]{0:T(128)S(1)} %multiply_bitcast_fusion), kind=kLoop, calls=%fused_computation.2 | loop fusion | flops 524288 | bytes 4456480 | tf_op jit(solution)/shard_map/sin | solution.py:198
  76.6 52.5 %all-gather.6.cloned.1.call-done = bf16[1,64,65536]{2,1,0:T(8,128)(2,1)} async-done(((bf16[1,16,65536]{2,1,0:T(8,128)(2,1)}), bf16[1,64,65536]{2,1,0:T(8,128)(2,1)}) %all-gather.6.cloned.1.call-update) | async-done | bytes 8388624 | tf_op jit(solution)/shard_map/all_gather | solution.py:183
  129.1 89.4 %all-gather.8.cloned.1.call-done = bf16[1,64,65536]{2,1,0:T(8,128)(2,1)} async-done(((bf16[1,16,65536]{2,1,0:T(8,128)(2,1)}), bf16[1,64,65536]{2,1,0:T(8,128)(2,1)}) %all-gather.8.cloned.1.call-update) | async-done | bytes 8388624 | tf_op jit(solution)/shard_map/all_gather | solution.py:183
  218.5 10.7 %shard_map.88 = f32[16,256,256]{2,1,0:T(8,128)} custom-call(bf16[2,16,64]{2,1,0:T(8,128)(2,1)} %pad_maximum_fusion.w_ref, bf16[64,65536]{1,0:T(8,128)(2,1)} %bitcast.29, bf16[64,65536]{1,0:T(8,128)(2,1)} %bitcast.30), custom_call_target="tpu_custom_call" | custom-call | flops 134217728 | bytes 8388608 | tf_op jit(solution)/shard_map/pallas_call | solution.py:54
  229.2 2.6 fusion.3
  231.8 0.1 multiply_dynamic-update-slice_fusion
  231.9 26.7 %shard_map.89 = f32[32,2,8,16,128]{4,3,2,1,0:T(8,128)} custom-call(f32[2,8,256,256]{3,2,1,0:T(8,128)} %bitcast.25, f32[8,256,256]{2,1,0:T(8,128)} %get-tuple-element.9.h_real_ref, f32[8,256,256]{2,1,0:T(8,128)} %get-tuple-element.8.h_imag_ref, bf16[2,512,512]{2,1,0:T(8,128)(2,1)} %constant.62.clone.left_ref, bf16[2,512,512]{2,1,0:T(8,128)(2,1)} %constant.63.clone.right_ref, ...), custom_call_target="tpu_custom_call" | custom-call | flops 12884901888 | bytes 12582912 | tf_op jit(solution)/shard_map/pallas_call | solution.py:152
  258.5 4.2 %multiply_convert_fusion = f16[32,2,8,16,128]{4,3,2,1,0:T(8,128)(2,1)} fusion(f32[32,2,8,16,128]{4,3,2,1,0:T(8,128)} %shard_map.89, f32[8]{0:T(128)S(1)} %get-tuple-element.13), kind=kLoop, calls=%fused_computation.1 | loop fusion | flops 2097152 | bytes 6291488 | tf_op jit(solution)/shard_map/convert_element_type | solution.py:203
  262.7 4.6 %all-to-all-start = ((f16[32,2,8,16,128]{4,3,2,1,0:T(8,128)(2,1)}), f16[32,2,8,16,128]{4,3,2,1,0:T(8,128)(2,1)S(1)}, u32[]{:S(2)}, u32[]{:S(2)}) async-start(f16[32,2,8,16,128]{4,3,2,1,0:T(8,128)(2,1)} %multiply_convert_fusion), calls=%async_computation | async-start | bytes 4194304 | tf_op jit(solution)/shard_map/all_to_all | solution.py:204
  267.3 69.7 %all-reduce = f32[256]{0:T(256)S(1)} all-reduce(f32[256]{0:T(256)S(1)} %get-tuple-element.12), channel_id=4, replica_groups=mesh['sub'=8,'sta'=4] {'sub','sta'}, use_global_device_ids=true, to_apply=%add | all-reduce | flops 256 | bytes 2048
  337.0 0.1 reshape.136
  337.1 0.0 all-to-all-done
  337.1 0.4 convert_multiply_fusion
  337.6 0.5 copy.10
  338.0 0.0 copy-start
  338.1 0.3 fusion.1
  338.4 1.7 copy-done
  340.1 0.7 broadcast_multiply_fusion
  (4 shorter events, 0.0 us)
Async XLA Ops:
  7.2 121.9 %all-gather.6.cloned.1.call-start = ((), (), s32[]{:S(2)}) async-start(), calls=%async_computation.1 | async-start | bytes 10485760 | tf_op jit(solution)/shard_map/all_gather | solution.py:183
  38.7 179.8 %all-gather.8.cloned.1.call-start = ((), (), s32[]{:S(2)}) async-start(), calls=%async_computation.2 | async-start | bytes 10485760 | tf_op jit(solution)/shard_map/all_gather | solution.py:183
  65.6 2.0 copy-start.1
  262.7 74.4 %all-to-all-start = ((f16[32,2,8,16,128]{4,3,2,1,0:T(8,128)(2,1)}), f16[32,2,8,16,128]{4,3,2,1,0:T(8,128)(2,1)S(1)}, u32[]{:S(2)}, u32[]{:S(2)}) async-start(f16[32,2,8,16,128]{4,3,2,1,0:T(8,128)(2,1)} %multiply_convert_fusion), calls=%async_computation | async-start | bytes 4194304 | tf_op jit(solution)/shard_map/all_to_all | solution.py:204
  338.0 2.0 copy-start
Sparse Core Ops, SparseCore 0:
  38.8 90.2 all-gather.5
  131.0 87.4 all-gather.7
